TPU v7x, 256 devices: a 4x2x16 block of a 4x16x16 slice. The times are simulated.
256 devices in a mesh: groups: 2 (over y), seq: 16 (over z), head: 8 (over x, core).
Axes of the slice: x: 4, y: 2, z: 16, core: 2. Of those that a mesh axis runs over, the one named last changes fastest.
The devices are a block of a 4x16x16 slice.
Arguments:
- residual: bfloat16 [16384, 2560], P(('groups', 'seq'), 'head'), parts along dimension 0, may hold values from -6 to 6
- x_in: bfloat16 [16384, 5120], P(('groups', 'seq'), 'head'), parts along dimension 0, may hold values from -6 to 6
- bc_in: bfloat16 [16384, 256], P(('groups', 'seq')), parts along dimension 0, may hold values from -1.5 to 1.5
- z_in: bfloat16 [16384, 5120], P(('groups', 'seq'), 'head'), parts along dimension 0, may hold values from -6 to 6
- dt_raw: float32 [80, 16384], P('head', ('groups', 'seq')), parts along dimension 1, may hold values from -5 to 5
- dt_bias: float32 [80], P('head'), may hold values from -3 to 0
- decay_rate: float32 [80], P('head'), may hold values from 0.0003 to 0.15
- d_skip: float32 [80], P('head'), may hold values from 1 to 4
- conv_x_weight: bfloat16 [4, 5120], P(None, 'head'), may hold values from -3 to 3
- conv_x_bias: bfloat16 [5120], P('head'), may hold values from -3 to 3
- conv_bc_weight: bfloat16 [4, 256], replicated, may hold values from -3 to 3
- conv_bc_bias: bfloat16 [256], replicated, may hold values from -3 to 3
- norm_gain: bfloat16 [5120], P('head'), may hold values from 0.5 to 1.5
- out_weight: bfloat16 [5120, 2560], P('head'), may hold values from -0.078125 to 0.078125
- final_gain: bfloat16 [2560], replicated, may hold values from 0.5 to 1.5
- lm_weight: bfloat16 [2560, 25600], P('seq', 'head'), may hold values from -15.811388 to 15.811388
- targets: int32 [16384], P(('groups', 'seq')), parts along dimension 0, may hold values from 0 to 25599
- doc_lengths: int32 [32], P('groups'), parts along dimension 0, may hold values from 1 to 1536, as said below
Outputs:
- block_out: bfloat16 [16384, 2560], P(('groups', 'seq'), 'head'), parts along dimension 0
- doc_loss: float32 [32], P('groups'), parts along dimension 0
There are 2 independent parts, one for each index of `groups`. A program takes and returns all parts, laid end to end along the dimension named above; an argument that names none is the same for every part. Nothing has to cross between parts.
Inputs may be any that keep to these rules, and one draw needn't show every extreme that they name: `doc_lengths`: the lengths of a group's 16 documents, in the order in which they are packed into its 8192 tokens; they sum to 8192.
All inputs are finite; a program needn't handle non-finite values.
Results may differ from a plain program's by a relative error of at most 0.00145.
The roundings to bfloat16 on the way count: a program that leaves them out, or rounds other values in their place, can miss the bound.
Values may be sent and summed in bfloat16 or wider, within the bound.
No kernel may reach another device: no remote copies, remote signals or barrier semaphores. Data moves between devices by JAX's collectives and lax.ppermute only.
A program may use at most 128 MiB of HBM per device.

v0:
```python
import jax
import jax.numpy as jnp
from jax import lax
from jax.sharding import PartitionSpec as P

D = 2560
HEAD_SIZE = 64
STATE = 128
KERNEL = 4
SPAN = 256
INNER = 5120
EPSILON = 1e-05
HIGH = lax.Precision.HIGHEST


def shifted(array, axis, by):
    length = lax.axis_size(axis)
    pairs = [(i, i + by) for i in range(length) if 0 <= i + by < length]
    return lax.ppermute(array, axis, pairs)


def entering(part, axis, combine, identity):
    place = lax.axis_index(axis)
    gathered = jax.tree.map(lambda a: lax.all_gather(a, axis), part)
    state = jax.tree.map(lambda a, e: jnp.zeros_like(a) + jnp.asarray(e, a.dtype), part, identity)

    def one(lap, state):
        return combine(
            state, jax.tree.map(lambda a: lax.dynamic_index_in_dim(a, lap, 0, False), gathered)
        )

    return lax.fori_loop(0, place, one, state)


def cut_along(array, dim, length):
    shape = array.shape
    blocks = array.reshape(*shape[:dim], length, shape[dim] // length, *shape[dim + 1 :])
    return jnp.moveaxis(blocks, dim, 0)


def sent_and_summed(array, axis, dim):
    blocks = cut_along(array, dim, lax.axis_size(axis))
    arrived = lax.all_to_all(blocks, axis, split_axis=0, concat_axis=0, tiled=True)
    return arrived.sum(axis=0)


def joined_along(blocks, dim):
    shape = list(blocks.shape[1:])
    shape[dim] *= blocks.shape[0]
    return jnp.moveaxis(blocks, 0, dim).reshape(shape)


def from_everyone(array, axis):
    length = lax.axis_size(axis)
    return lax.all_to_all(
        jnp.broadcast_to(array[None], (length, *array.shape)), axis, 0, 0, tiled=True
    )


def gather_directly(array, axis, dim):
    return joined_along(from_everyone(array, axis), dim)


def gathered_once(array, axis):
    leaves = jax.tree.leaves(array)
    sequence = sorted(range(len(leaves)), key=lambda k: -leaves[k].size)
    width = (1, *leaves[sequence[0]].shape)[-1]
    lines = [
        jnp.pad(leaves[k].reshape(-1), (0, -leaves[k].size % width)).reshape(-1, width)
        for k in sequence
    ]
    both, at, found = (lax.all_gather(jnp.concatenate(lines), axis), 0, {})
    for k, line in zip(sequence, lines):
        section = both[:, at : at + len(line)].reshape(len(both), -1)
        found[k] = section[:, : leaves[k].size].reshape(-1, *leaves[k].shape)
        at += len(line)
    numbers = iter(range(len(leaves)))
    return jax.tree.map(lambda _: found[next(numbers)], array)


def joined_2(part, axis, combine):
    gathered = gathered_once(part, axis)

    def take(source):
        return jax.tree.map(lambda a: lax.dynamic_index_in_dim(a, source, 0, False), gathered)

    return lax.fori_loop(
        1, lax.axis_size(axis), lambda source, state: combine(state, take(source)), take(0)
    )


def over_copies(array, axis):
    return from_everyone(array, axis).sum(axis=0)


def document_of(positions, doc_lengths):
    starts = jnp.cumsum(doc_lengths) - doc_lengths
    return jnp.sum((positions[:, None] >= starts[None, :]).astype(jnp.int32), axis=1) - 1


def causal_conv(signal, rim_rows, weight, bias, positions, doc_ids, doc_lengths):
    length = signal.shape[0]
    taps = weight.shape[0]
    joined = jnp.concatenate([rim_rows, signal], axis=0).astype(jnp.float32)
    total = jnp.zeros(signal.shape, jnp.float32) + bias.astype(jnp.float32)[None, :]
    for offset in range(taps):
        lag = taps - 1 - offset
        source = document_of(positions - lag, doc_lengths)
        same = (source == doc_ids).astype(jnp.float32)
        total = (
            total
            + weight[offset].astype(jnp.float32)[None, :]
            * joined[offset : offset + length]
            * same[:, None]
        )
    return jax.nn.silu(total).astype(jnp.bfloat16)


def span_step(state, pieces, rates):
    signal, bmat, cmat, steps, doc_ids, doc_prev = pieces
    signal = signal.astype(jnp.float32)
    bmat = bmat.astype(jnp.float32)
    cmat = cmat.astype(jnp.float32)
    climb = jnp.cumsum(steps * rates[:, None], axis=1)
    extent = doc_ids.shape[0]
    order = jnp.arange(extent, dtype=jnp.int32)
    inside = (doc_ids[:, None] == doc_ids[None, :]) & (order[:, None] >= order[None, :])
    gap = climb[:, :, None] - climb[:, None, :]
    decay = jnp.where(inside[None], jnp.exp(-jnp.where(inside[None], gap, 0.0)), 0.0)
    scores = jnp.dot(cmat, bmat.T, precision=HIGH)
    weights = decay * scores[None] * steps[:, None, :]
    output = jnp.einsum("hts,shp->thp", weights, signal, precision=HIGH)
    carried = (doc_ids == doc_prev).astype(jnp.float32)
    entry = jnp.exp(-climb) * carried[None, :]
    output = output + jnp.einsum("tn,hpn->thp", cmat, state, precision=HIGH) * entry.T[:, :, None]
    last = doc_ids[extent - 1]
    tail = (
        jnp.exp(climb - climb[:, extent - 1 :])
        * (doc_ids == last).astype(jnp.float32)[None, :]
        * steps
    )
    kept = jnp.exp(-climb[:, extent - 1]) * (last == doc_prev).astype(jnp.float32)
    fresh = jnp.einsum("hs,shp,sn->hpn", tail, signal, bmat, precision=HIGH)
    return (kept[:, None, None] * state + fresh, output)


def chain_combine(earlier, later):
    return (earlier[0] * later[0], later[0][:, None, None] * earlier[1] + later[1])


def softmax_combine(first_part, second_part):
    peak = jnp.maximum(first_part[0], second_part[0])
    total = first_part[1] * jnp.exp(first_part[0] - peak) + second_part[1] * jnp.exp(
        second_part[0] - peak
    )
    return (peak, total, first_part[2] + second_part[2])


def local(
    residual,
    x_in,
    bc_in,
    z_in,
    dt_raw,
    dt_bias,
    decay_rate,
    d_skip,
    conv_x_weight,
    conv_x_bias,
    conv_bc_weight,
    conv_bc_bias,
    norm_gain,
    out_weight,
    final_gain,
    lm_weight,
    targets,
    doc_lengths,
):
    length = x_in.shape[0]
    inner_here = x_in.shape[1]
    heads_here = dt_raw.shape[0]
    seq_rank = lax.axis_index("seq")
    head_rank = lax.axis_index("head")
    offset_here = seq_rank * length
    positions = offset_here + jnp.arange(length, dtype=jnp.int32)
    doc_ids = document_of(positions, doc_lengths)
    margin = KERNEL - 1
    x_rim, bc_rim = shifted((x_in[length - margin :], bc_in[length - margin :]), "seq", 1)
    signal = causal_conv(x_in, x_rim, conv_x_weight, conv_x_bias, positions, doc_ids, doc_lengths)
    keys_queries = causal_conv(
        bc_in, bc_rim, conv_bc_weight, conv_bc_bias, positions, doc_ids, doc_lengths
    )
    steps = jax.nn.softplus(dt_raw + dt_bias[:, None])
    blocks = length // SPAN
    block_starts = offset_here + jnp.arange(blocks, dtype=jnp.int32) * SPAN
    pieces = (
        signal.reshape(blocks, SPAN, heads_here, HEAD_SIZE),
        keys_queries[:, :STATE].reshape(blocks, SPAN, STATE),
        keys_queries[:, STATE:].reshape(blocks, SPAN, STATE),
        steps.reshape(heads_here, blocks, SPAN).transpose(1, 0, 2),
        doc_ids.reshape(blocks, SPAN),
        document_of(block_starts - 1, doc_lengths),
    )

    def advance(state, piece):
        return span_step(state, piece, decay_rate)

    local_end, outputs = lax.scan(
        advance, jnp.zeros((heads_here, HEAD_SIZE, STATE), jnp.float32), pieces
    )
    outputs = outputs.reshape(length, heads_here, HEAD_SIZE)
    before = document_of(jnp.reshape(offset_here - 1, (1,)), doc_lengths)[0]
    carried = (doc_ids == before).astype(jnp.float32)
    climb = jnp.cumsum(steps * decay_rate[:, None], axis=1)
    through = jnp.exp(-climb[:, length - 1]) * carried[length - 1]
    identity = (jnp.ones_like(through), jnp.zeros_like(local_end))
    incoming = entering((through, local_end), "seq", chain_combine, identity)[1]
    entry = jnp.exp(-climb) * carried[None, :]
    cmat = keys_queries[:, STATE:].astype(jnp.float32)
    outputs = (
        outputs + jnp.einsum("tn,hpn->thp", cmat, incoming, precision=HIGH) * entry.T[:, :, None]
    )
    mixed = outputs + d_skip[None, :, None] * signal.reshape(length, heads_here, HEAD_SIZE).astype(
        jnp.float32
    )
    gated = mixed.reshape(length, inner_here) * jax.nn.silu(z_in.astype(jnp.float32))
    square_sum = lax.psum(jnp.sum(gated * gated, axis=1), "head")
    scale = lax.rsqrt(square_sum / INNER + EPSILON)
    normed = (gated * scale[:, None] * norm_gain.astype(jnp.float32)[None, :]).astype(jnp.bfloat16)
    partial_value = jnp.dot(normed, out_weight, preferred_element_type=jnp.float32)
    share = residual.shape[1]
    projected = sent_and_summed(partial_value, "head", 1)
    block_out = (residual.astype(jnp.float32) + projected).astype(jnp.bfloat16)
    widened = block_out.astype(jnp.float32)
    square_total = lax.psum(jnp.sum(widened * widened, axis=1), "head")
    gain_part = lax.dynamic_slice_in_dim(final_gain, head_rank * share, share, 0)
    final_scale = lax.rsqrt(square_total / D + EPSILON)
    hidden_part = (widened * final_scale[:, None] * gain_part.astype(jnp.float32)[None, :]).astype(
        jnp.bfloat16
    )
    hidden = gather_directly(hidden_part, "head", 1)
    vocab_here = lm_weight.shape[1]
    logits = jnp.dot(
        hidden,
        lax.all_gather(lm_weight, "seq", axis=0, tiled=True),
        preferred_element_type=jnp.float32,
    )
    peak = jnp.max(logits, axis=1)
    total = jnp.sum(jnp.exp(logits - peak[:, None]), axis=1)
    local_target = targets - head_rank * vocab_here
    column = jnp.arange(vocab_here, dtype=jnp.int32)
    picked = jnp.sum(jnp.where(column[None, :] == local_target[:, None], logits, 0.0), axis=1)
    peak_all, total_all, picked_all = joined_2((peak, total, picked), "head", softmax_combine)
    losses = peak_all + jnp.log(total_all) - picked_all
    member = (
        doc_ids[:, None] == jnp.arange(doc_lengths.shape[0], dtype=jnp.int32)[None, :]
    ).astype(jnp.float32)
    sums = over_copies(jnp.dot(losses, member, precision=HIGH), "seq")
    return (block_out, sums / doc_lengths.astype(jnp.float32))


def solution(mesh):
    in_specs = (
        P(("groups", "seq"), "head"),
        P(("groups", "seq"), "head"),
        P(("groups", "seq"), None),
        P(("groups", "seq"), "head"),
        P("head", ("groups", "seq")),
        P("head"),
        P("head"),
        P("head"),
        P(None, "head"),
        P("head"),
        P(),
        P(),
        P("head"),
        P("head", None),
        P(),
        P("seq", "head"),
        P(("groups", "seq")),
        P("groups"),
    )
    out_specs = (P(("groups", "seq"), "head"), P("groups"))
    return jax.shard_map(local, mesh=mesh, in_specs=in_specs, out_specs=out_specs, check_vma=False)
```

profile of v0, /device:TPU:33, one launch (start us, length us, event | category | flops | bytes accessed | tf_op | source)
XLA Modules:
  0.0 454.0 jit_solution(4214907796771070101)
XLA Ops:
  8.7 5.8 %collective-permute-start = (bf16[3,640]{1,0:T(4,128)(2,1)}, bf16[3,640]{1,0:T(4,128)(2,1)}, u32[]{:S(2)}, u32[]{:S(2)}) collective-permute-start(bf16[3,640]{1,0:T(4,128)(2,1)} %slice.103), channel_id=1, source_target_pairs={{0,8},{8,16},{16,24},{24,32},{32,40},{40,48},{48,56},{56,64},{64,7... | collective-permute-start | bytes 11528 | tf_op jit(solution)/shard_map/ppermute | solution.py:19
  15.2 3.8 collective-permute-start.1
  34.5 2.2 copy.83
  36.7 2.7 reshape.293
  39.4 2.1 copy.85
  41.5 80.0 %while.46 = (s32[]{:T(128)}, f32[10,64,128]{2,1,0:T(8,128)}, f32[2,256,10,64]{1,0,3,2:T(2,128)}, f32[2,10,256]{2,0,1:T(2,128)}, f32[10]{0:T(128)}, /*index=5*/s3...) while((s32[]{:T(128)}, f32[10,64,128]{2,1,0:T(8,128)}, ...), condition=%wide.region_9.10_spmd.clone, body=%wide.region_6.9_spmd.clone.sunk | while | flops 1028866112 | bytes 7581990 | solution.py:208
  51.7 4.0 fusion.117
  63.0 14.2 %dynamic_update_slice.6 = f32[2,256,10,64]{1,0,3,2:T(2,128)} dynamic-update-slice(f32[2,256,10,64]{1,0,3,2:T(2,128)} %get-tuple-element.624, f32[1,256,10,64]{1,0,3,2:T(1,128)} %copy.129, s32[]{:T(128)} %get-tuple-element.622, s32[]{:T(128)} %constant.152.clone.1..sunk.2, s32[]{:T(128)} %constant.152.clone.1..sunk.2, s32[]{:T(128)} %constant.152.clone.1..sunk.2) | dynamic-update-slice | bytes 1310724 | tf_op jit(solution)/shard_map/while/body/jit(dynamic_update_index_in_dim)/dynamic_update_slice | solution.py:208
  79.2 2.2 convolution_add_fusion.2
  91.6 4.0 fusion.117
  103.0 14.2 %dynamic_update_slice.6 = f32[2,256,10,64]{1,0,3,2:T(2,128)} dynamic-update-slice(f32[2,256,10,64]{1,0,3,2:T(2,128)} %get-tuple-element.624, f32[1,256,10,64]{1,0,3,2:T(1,128)} %copy.129, s32[]{:T(128)} %get-tuple-element.622, s32[]{:T(128)} %constant.152.clone.1..sunk.2, s32[]{:T(128)} %constant.152.clone.1..sunk.2, s32[]{:T(128)} %constant.152.clone.1..sunk.2) | dynamic-update-slice | bytes 1310724 | tf_op jit(solution)/shard_map/while/body/jit(dynamic_update_index_in_dim)/dynamic_update_slice | solution.py:208
  119.2 2.3 convolution_add_fusion.2
  126.8 39.9 %all-reduce = f32[160]{0:T(256)S(1)} all-reduce(f32[160]{0:T(256)S(1)} %dynamic-update-slice), channel_id=2, replica_groups=mesh['groups'=2,'seq'=16,'head'=8] {'seq'}, use_global_device_ids=true, to_apply=%add | all-reduce | flops 160 | bytes 1280
  167.4 2.4 copy.89
  169.8 3.2 reshape.296
  173.0 32.3 %all-gather.9.cloned.1.call-done = f32[160,64,128]{2,1,0:T(8,128)} async-done(((f32[10,64,128]{2,1,0:T(8,128)}), f32[160,64,128]{2,1,0:T(8,128)}) %all-gather.9.cloned.1.call-update) | async-done | bytes 5242896 | tf_op jit(solution)/shard_map/all_gather | solution.py:24
  207.0 3.7 fusion.46
  210.8 2.8 copy.90
  213.6 2.0 multiply_reduce_fusion
  215.5 20.6 %psum.14 = f32[512]{0:T(512)S(1)} all-reduce(f32[512]{0:T(512)S(1)} %multiply_reduce_fusion), channel_id=1, replica_groups=mesh['groups'=2,'seq'=16,'head'=8] {'head'}, use_global_device_ids=true, to_apply=%region_16.17 | all-reduce | flops 512 | bytes 4096 | tf_op jit(solution)/shard_map/psum | solution.py:227
  236.2 6.4 %fusion.61 = f32[512,2560]{0,1:T(8,128)} fusion(bf16[640,2560]{1,0:T(8,128)(2,1)S(1)} %copy-done, f32[640]{0:T(1024)S(1)} %convert_element_type.158, f32[512]{0:T(512)S(1)} %add_rsqrt_fusion.1, f32[512,640]{1,0:T(8,128)} %copy.90, bf16[512,640]{1,0:T(8,128)(2,1)} %param.27), kind=kOutput, calls=%fused_computation.97 | convolution fusion | flops 1680670720 | bytes 10490368 | tf_op jit(solution)/shard_map/dot_general | solution.py:230
  242.5 5.2 %all-to-all-start = ((f32[8,512,320]{1,2,0:T(8,128)}), f32[8,512,320]{1,2,0:T(8,128)}, u32[]{:S(2)}, u32[]{:S(2)}) async-start(f32[8,512,320]{1,2,0:T(8,128)} %bitcast.151), calls=%async_computation | async-start | bytes 10485760 | tf_op jit(solution)/shard_map/all_to_all | solution.py:43
  248.5 59.3 %all-to-all-done = f32[8,512,320]{1,2,0:T(8,128)} async-done(((f32[8,512,320]{1,2,0:T(8,128)}), f32[8,512,320]{1,2,0:T(8,128)}, u32[]{:S(2)}, u32[]{:S(2)}) %all-to-all-start) | async-done | bytes 5242912 | tf_op jit(solution)/shard_map/all_to_all | solution.py:43
  307.9 4.0 reduce_sum.118
  311.9 2.0 fusion.58
  313.9 13.2 %psum.15 = f32[512]{0:T(512)S(1)} all-reduce(f32[512]{0:T(512)S(1)} %get-tuple-element.424), channel_id=1, replica_groups=mesh['groups'=2,'seq'=16,'head'=8] {'head'}, use_global_device_ids=true, to_apply=%region_19.20 | all-reduce | flops 512 | bytes 4096 | tf_op jit(solution)/shard_map/psum | solution.py:235
  329.9 5.8 %all-to-all-start.1 = ((bf16[8,512,320]{1,2,0:T(8,128)(2,1)}), bf16[8,512,320]{1,2,0:T(8,128)(2,1)}, u32[]{:S(2)}, u32[]{:S(2)}) async-start(bf16[8,512,320]{1,2,0:T(8,128)(2,1)} %broadcast_in_dim.26), calls=%async_computation.1 | async-start | bytes 5242880 | tf_op jit(solution)/shard_map/all_to_all | solution.py:55
  335.7 32.0 %all-to-all-done.1 = bf16[8,512,320]{1,2,0:T(8,128)(2,1)} async-done(((bf16[8,512,320]{1,2,0:T(8,128)(2,1)}), bf16[8,512,320]{1,2,0:T(8,128)(2,1)}, u32[]{:S(2)}, u32[]{:S(2)}) %all-to-all-start.1) | async-done | bytes 2621472 | tf_op jit(solution)/shard_map/all_to_all | solution.py:55
  367.7 27.6 %all-gather.7.cloned.1.call-done = bf16[2560,3200]{1,0:T(8,128)(2,1)} async-done(((bf16[160,3200]{1,0:T(8,128)(2,1)}), bf16[2560,3200]{1,0:T(8,128)(2,1)}) %all-gather.7.cloned.1.call-update) | async-done | bytes 16384016 | tf_op jit(solution)/shard_map/all_gather | solution.py:245
  395.3 14.5 %fusion.89 = (f32[512]{0:T(512)S(1)}, f32[512,3200]{1,0:T(8,128)S(1)}) fusion(bf16[512,2560]{0,1:T(8,128)(2,1)} %bitcast.23, bf16[2560,3200]{1,0:T(8,128)(2,1)} %all-gather.7.cloned.1.call-done), kind=kOutput, calls=%fused_computation.170 | convolution fusion | flops 8390245888 | bytes 25561088 | tf_op jit(solution)/shard_map/dot_general | solution.py:243
  411.8 13.9 %all-gather.3 = f32[8,3,512]{2,1,0:T(4,128)S(1)} all-gather(f32[1,3,512]{2,1,0:T(4,128)S(1)} %maximum_bitcast_fusion), channel_id=4, replica_groups=mesh['groups'=2,'seq'=16,'head'=8] {'head'}, dimensions={0}, use_global_device_ids=true | all-gather | bytes 55296 | tf_op jit(solution)/shard_map/all_gather | solution.py:72
  426.8 19.8 %all_to_all.16 = f32[16,1,16]{2,1,0:T(1,128)S(1)} all-to-all(f32[16,1,16]{2,1,0:T(1,128)S(1)} %broadcast_in_dim.28), channel_id=1, replica_groups=mesh['groups'=2,'seq'=16,'head'=8] {'seq'}, dimensions={0} | all-to-all | bytes 2048 | tf_op jit(solution)/shard_map/all_to_all | solution.py:55
  (193 shorter events, 67.5 us)
Async XLA Ops:
  7.2 229.0 %copy-start = (bf16[640,2560]{1,0:T(8,128)(2,1)S(1)}, bf16[640,2560]{1,0:T(8,128)(2,1)}, u32[]{:S(2)}) copy-start(bf16[640,2560]{1,0:T(8,128)(2,1)} %param.37) | copy-start | bytes 9830404
  7.2 198.1 %all-gather.9.cloned.1.call-start = ((), (), s32[]{:S(2)}) async-start(), calls=%async_computation.4 | async-start | bytes 5570560 | tf_op jit(solution)/shard_map/all_gather | solution.py:24
  8.7 23.1 %collective-permute-start = (bf16[3,640]{1,0:T(4,128)(2,1)}, bf16[3,640]{1,0:T(4,128)(2,1)}, u32[]{:S(2)}, u32[]{:S(2)}) collective-permute-start(bf16[3,640]{1,0:T(4,128)(2,1)} %slice.103), channel_id=1, source_target_pairs={{0,8},{8,16},{16,24},{24,32},{32,40},{40,48},{48,56},{56,64},{64,7... | collective-permute-start | bytes 11528 | tf_op jit(solution)/shard_map/ppermute | solution.py:19
  15.2 14.4 %collective-permute-start.1 = (bf16[3,256]{1,0:T(4,128)(2,1)S(1)}, bf16[3,256]{1,0:T(4,128)(2,1)S(1)}, u32[]{:S(2)}, u32[]{:S(2)}) collective-permute-start(bf16[3,256]{1,0:T(4,128)(2,1)S(1)} %slice.112), channel_id=1, source_target_pairs={{0,8},{8,16},{16,24},{24,32},{32,40},{40,48},{48,56},{56,64},{64,7... | collective-permute-start | bytes 4616 | tf_op jit(solution)/shard_map/ppermute | solution.py:19
  22.9 7.7 %copy-start.13 = (s32[512]{0:T(512)}, s32[512]{0:T(512)S(1)}, u32[]{:S(2)}) copy-start(s32[512]{0:T(512)S(1)} %broadcast_add_fusion.2) | copy-start | bytes 6148
  30.7 1.1 copy-start.5
  31.1 0.7 copy-start.3
  31.1 1.5 copy-start.8
  31.1 1.5 copy-start.9
  31.1 1.5 copy-start.10
  31.1 1.5 copy-start.11
  48.3 3.4 copy-start.1
  58.6 1.4 copy-start.7
  61.5 17.7 %copy-start.2 = (f32[256,10]{0,1:T(8,128)S(1)}, f32[256,10]{0,1:T(8,128)}, u32[]{:S(2)}) copy-start(f32[256,10]{0,1:T(8,128)} %get-tuple-element.606) | copy-start | bytes 30724 | tf_op jit(solution)/shard_map/while
  88.1 3.4 copy-start.1
  98.5 1.4 copy-start.7
  101.5 17.7 %copy-start.2 = (f32[256,10]{0,1:T(8,128)S(1)}, f32[256,10]{0,1:T(8,128)}, u32[]{:S(2)}) copy-start(f32[256,10]{0,1:T(8,128)} %get-tuple-element.606) | copy-start | bytes 30724 | tf_op jit(solution)/shard_map/while
  121.4 0.9 copy-start.12
  121.4 1.5 copy-start.6
  121.4 3.0 copy-start.19
  121.4 45.3 %copy-start.15 = (bf16[640]{0:T(1024)(128)(2,1)S(1)}, bf16[640]{0:T(1024)(128)(2,1)}, u32[]{:S(2)}) copy-start(bf16[640]{0:T(1024)(128)(2,1)} %param.36) | copy-start | bytes 3844
  121.5 273.8 %all-gather.7.cloned.1.call-start = ((), (), s32[]{:S(2)}) async-start(), calls=%async_computation.3 | async-start | bytes 17408000 | tf_op jit(solution)/shard_map/all_gather | solution.py:245
  206.1 0.9 copy-start.4
  206.1 1.0 copy-start.18
  242.5 65.3 %all-to-all-start = ((f32[8,512,320]{1,2,0:T(8,128)}), f32[8,512,320]{1,2,0:T(8,128)}, u32[]{:S(2)}, u32[]{:S(2)}) async-start(f32[8,512,320]{1,2,0:T(8,128)} %bitcast.151), calls=%async_computation | async-start | bytes 10485760 | tf_op jit(solution)/shard_map/all_to_all | solution.py:43
  329.9 5.8 %copy-start.17 = (s32[512]{0:T(512)S(1)}, s32[512]{0:T(512)}, u32[]{:S(2)}) copy-start(s32[512]{0:T(512)} %param.40) | copy-start | bytes 6148
  329.9 37.8 %all-to-all-start.1 = ((bf16[8,512,320]{1,2,0:T(8,128)(2,1)}), bf16[8,512,320]{1,2,0:T(8,128)(2,1)}, u32[]{:S(2)}, u32[]{:S(2)}) async-start(bf16[8,512,320]{1,2,0:T(8,128)(2,1)} %broadcast_in_dim.26), calls=%async_computation.1 | async-start | bytes 5242880 | tf_op jit(solution)/shard_map/all_to_all | solution.py:55
  409.8 16.7 %copy-start.14 = (s32[512]{0:T(512)S(1)}, s32[512]{0:T(512)}, u32[]{:S(2)}) copy-start(s32[512]{0:T(512)} %copy-done.13) | copy-start | bytes 6148
  409.8 36.8 %copy-start.16 = (s32[16]{0:T(128)S(1)}, s32[16]{0:T(128)}, u32[]{:S(2)}) copy-start(s32[16]{0:T(128)} %param.41) | copy-start | bytes 196
Sparse Core Ops, SparseCore 0:
  121.6 83.6 all-gather.8
  207.1 188.1 all-gather.6
where the time goes:
time: 458 us; the launch traced here: 454 us
  waiting for transfers between devices  152 us (33%)
  blocking collectives  107 us (23%)
  local copies, waits for them, and re-layouts  69.2 us (15%)
  other arithmetic  44.6 us (10%)
  matrix products  40.9 us (9%)
  starting transfers between devices  20.8 us (5%)
  between operations  15.8 us (3%)
    all_to_all x1, waiting for transfers between devices, sent_and_summed(): lax.all_to_all(blocks, axis, split_axis=0, concat_axis=0, tiled=True)  59.3 us
    unnamed x1, blocking collectives  39.9 us
    all_gather x1, waiting for transfers between devices, entering(): gathered = jax.tree.map(lambda a: lax.all_gather(a, axis), part)  32.3 us
    all_to_all x1, waiting for transfers between devices, from_everyone(): lax.all_to_all(jnp.broadcast_to(array[None], (length, *array.shape)), axi...  32 us
    dynamic_update_slice x4, local copies, waits for them, and re-layouts, local(): lax.scan(advance, jnp.zeros((heads_here, HEAD_SIZE, STATE), jnp.float32),...  31.3 us
    all_gather x1, waiting for transfers between devices, local(): lax.all_gather(lm_weight, 'seq', axis=0, tiled=True)  27.6 us
    psum x1, blocking collectives, local(): square_sum = lax.psum(jnp.sum(gated * gated, axis=1), 'head')  20.6 us
    all_to_all x1, blocking collectives, from_everyone(): lax.all_to_all(jnp.broadcast_to(array[None], (length, *array.shape)), axi...  19.8 us
  transfers between devices with their start and end apart: 6, of which 4 were waited for; matrix products, arithmetic and copies ran while one was open for 10% of the time, Pallas kernels for 0%

commit v1 on v0

--- a/solution.py
+++ b/solution.py
@@ -1,3 +1,4 @@
+import functools
 import jax
 import jax.numpy as jnp
 from jax import lax
@@ -11,6 +12,21 @@
 INNER = 5120
 EPSILON = 1e-05
 HIGH = lax.Precision.HIGHEST
+
+
+def table_wait(mine_x, mesh_ax):
+    n_axis = lax.axis_size(mesh_ax)
+    ii = 0
+    steps_seen = []
+    while ii < mine_x.ndim:
+        steps_seen.append(n_axis if ii == 0 else 1)
+        ii = ii + 1
+    state_next = jnp.tile(mine_x, steps_seen)
+    formed = lax.all_to_all(state_next, mesh_ax, split_axis=0, concat_axis=0, tiled=True)
+    return formed
+
+
+trace_figure = functools.partial(table_wait, mesh_ax="seq")
 
 
 def shifted(array, axis, by):
@@ -240,11 +256,7 @@
     )
     hidden = gather_directly(hidden_part, "head", 1)
     vocab_here = lm_weight.shape[1]
-    logits = jnp.dot(
-        hidden,
-        lax.all_gather(lm_weight, "seq", axis=0, tiled=True),
-        preferred_element_type=jnp.float32,
-    )
+    logits = jnp.dot(hidden, trace_figure(lm_weight), preferred_element_type=jnp.float32)
     peak = jnp.max(logits, axis=1)
     total = jnp.sum(jnp.exp(logits - peak[:, None]), axis=1)
     local_target = targets - head_rank * vocab_here

time: 458 us -> 1170 us (2.55)
  waiting for transfers between devices: 152 us -> 794 us
  blocking collectives: 107 us -> 144 us
  starting transfers between devices: 20.8 us -> 46.1 us
    all_to_all x1, waiting for transfers between devices: 32 us -> 704 us  [table_wait(): lax.all_to_all(state_next, mesh_ax, split_axis=0, concat_axis=0, tiled=True)]
    all_to_all x1 -> x2, blocking collectives: 19.8 us -> 57.9 us  [from_everyone(): lax.all_to_all(jnp.broadcast_to(array[None], (length, *array.shape)), axi...]
    all_gather x1 -> x0, waiting for transfers between devices: 27.6 us -> none  [local(): lax.all_gather(lm_weight, 'seq', axis=0, tiled=True)]
    all_to_all x1, starting transfers between devices: 5.77 us -> 31.3 us  [table_wait(): lax.all_to_all(state_next, mesh_ax, split_axis=0, concat_axis=0, tiled=True)]
  transfers between devices with their start and end apart: 6 -> 5, of which waited for: 4 -> 3; matrix products, arithmetic and copies ran while one was open for 10% -> 2% of each run, Pallas kernels for 0% -> 0%
where the time goes in v1:
time: 1170 us; the launch traced here: 1160 us
  waiting for transfers between devices  794 us (68%)
  blocking collectives  144 us (12%)
  local copies, waits for them, and re-layouts  76 us (6%)
  starting transfers between devices  46.1 us (4%)
  other arithmetic  42.6 us (4%)
  matrix products  40.1 us (3%)
  between operations  15.8 us (1%)
    all_to_all x1, waiting for transfers between devices, table_wait(): lax.all_to_all(state_next, mesh_ax, split_axis=0, concat_axis=0, tiled=True)  704 us
    all_to_all x1, waiting for transfers between devices, sent_and_summed(): lax.all_to_all(blocks, axis, split_axis=0, concat_axis=0, tiled=True)  59.3 us
    all_to_all x2, blocking collectives, from_everyone(): lax.all_to_all(jnp.broadcast_to(array[None], (length, *array.shape)), axi...  57.9 us
    unnamed x1, blocking collectives  39.5 us
    dynamic_update_slice x4, local copies, waits for them, and re-layouts, local(): lax.scan(advance, jnp.zeros((heads_here, HEAD_SIZE, STATE), jnp.float32),...  31.3 us
    all_to_all x1, starting transfers between devices, table_wait(): lax.all_to_all(state_next, mesh_ax, split_axis=0, concat_axis=0, tiled=True)  31.3 us
    all_gather x1, waiting for transfers between devices, entering(): gathered = jax.tree.map(lambda a: lax.all_gather(a, axis), part)  30.4 us
  transfers between devices with their start and end apart: 5, of which 3 were waited for; matrix products, arithmetic and copies ran while one was open for 2% of the time, Pallas kernels for 0%

profile of v1, /device:TPU:33, one launch (start us, length us, event | category | flops | bytes accessed | tf_op | source)
XLA Modules:
  0.0 1161.7 jit_solution(10600358815875827660)
XLA Ops:
  8.7 5.8 collective-permute-start
  15.2 3.8 collective-permute-start.1
  34.7 2.2 copy.83
  36.9 2.7 reshape.300
  39.5 2.0 copy.85
  41.6 80.2 %while.46 = (s32[]{:T(128)}, f32[10,64,128]{2,1,0:T(8,128)}, f32[2,256,10,64]{1,0,3,2:T(2,128)}, f32[2,10,256]{2,0,1:T(2,128)}, f32[10]{0:T(128)}, /*index=5*/s3...) while((s32[]{:T(128)}, f32[10,64,128]{2,1,0:T(8,128)}, ...), condition=%wide.region_9.10_spmd.clone, body=%wide.region_6.9_spmd.clone.sunk | while | flops 1028866112 | bytes 7581990 | solution.py:224
  52.1 4.0 fusion.117
  63.3 14.2 %dynamic_update_slice.6 = f32[2,256,10,64]{1,0,3,2:T(2,128)} dynamic-update-slice(f32[2,256,10,64]{1,0,3,2:T(2,128)} %get-tuple-element.624, f32[1,256,10,64]{1,0,3,2:T(1,128)} %copy.129, s32[]{:T(128)} %get-tuple-element.622, s32[]{:T(128)} %constant.152.clone.1..sunk.2, s32[]{:T(128)} %constant.152.clone.1..sunk.2, s32[]{:T(128)} %constant.152.clone.1..sunk.2) | dynamic-update-slice | bytes 1310724 | tf_op jit(solution)/shard_map/while/body/jit(dynamic_update_index_in_dim)/dynamic_update_slice | solution.py:224
  79.4 2.2 convolution_add_fusion.2
  92.1 4.0 fusion.117
  103.4 14.2 %dynamic_update_slice.6 = f32[2,256,10,64]{1,0,3,2:T(2,128)} dynamic-update-slice(f32[2,256,10,64]{1,0,3,2:T(2,128)} %get-tuple-element.624, f32[1,256,10,64]{1,0,3,2:T(1,128)} %copy.129, s32[]{:T(128)} %get-tuple-element.622, s32[]{:T(128)} %constant.152.clone.1..sunk.2, s32[]{:T(128)} %constant.152.clone.1..sunk.2, s32[]{:T(128)} %constant.152.clone.1..sunk.2) | dynamic-update-slice | bytes 1310724 | tf_op jit(solution)/shard_map/while/body/jit(dynamic_update_index_in_dim)/dynamic_update_slice | solution.py:224
  119.5 2.3 convolution_add_fusion.2
  128.4 39.5 %all-reduce = f32[160]{0:T(256)S(1)} all-reduce(f32[160]{0:T(256)S(1)} %dynamic-update-slice), channel_id=2, replica_groups=mesh['groups'=2,'seq'=16,'head'=8] {'seq'}, use_global_device_ids=true, to_apply=%add | all-reduce | flops 160 | bytes 1280
  170.0 2.4 copy.89
  172.4 3.3 reshape.303
  175.7 30.4 %all-gather.6.cloned.1.call-done = f32[160,64,128]{2,1,0:T(8,128)} async-done(((f32[10,64,128]{2,1,0:T(8,128)}), f32[160,64,128]{2,1,0:T(8,128)}) %all-gather.6.cloned.1.call-update) | async-done | bytes 5242896 | tf_op jit(solution)/shard_map/all_gather | solution.py:40
  207.8 3.8 fusion.46
  211.6 2.8 copy.90
  214.4 2.0 multiply_reduce_fusion
  216.4 19.8 %psum.14 = f32[512]{0:T(512)S(1)} all-reduce(f32[512]{0:T(512)S(1)} %multiply_reduce_fusion), channel_id=1, replica_groups=mesh['groups'=2,'seq'=16,'head'=8] {'head'}, use_global_device_ids=true, to_apply=%region_16.17 | all-reduce | flops 512 | bytes 4096 | tf_op jit(solution)/shard_map/psum | solution.py:243
  236.2 6.3 fusion.61
  242.5 5.0 all-to-all-start
  248.4 59.3 %all-to-all-done = f32[8,512,320]{1,2,0:T(8,128)} async-done(((f32[8,512,320]{1,2,0:T(8,128)}), f32[8,512,320]{1,2,0:T(8,128)}, u32[]{:S(2)}, u32[]{:S(2)}) %all-to-all-start) | async-done | bytes 5242912 | tf_op jit(solution)/shard_map/all_to_all | solution.py:59
  307.7 3.2 reduce_sum.118
  311.0 12.8 %psum.15 = f32[512]{0:T(512)S(1)} all-reduce(f32[512]{0:T(512)S(1)} %get-tuple-element.424), channel_id=1, replica_groups=mesh['groups'=2,'seq'=16,'head'=8] {'head'}, use_global_device_ids=true, to_apply=%region_19.20 | all-reduce | flops 512 | bytes 4096 | tf_op jit(solution)/shard_map/psum | solution.py:251
  324.2 36.1 %all_to_all.25 = bf16[8,512,320]{1,2,0:T(8,128)(2,1)} all-to-all(bf16[8,512,320]{1,2,0:T(8,128)(2,1)S(1)} %broadcast_in_dim.26), channel_id=1, replica_groups=mesh['groups'=2,'seq'=16,'head'=8] {'head'}, dimensions={0} | all-to-all | bytes 5242880 | tf_op jit(solution)/shard_map/all_to_all | solution.py:71
  360.3 5.8 tile.2
  366.1 31.3 %all-to-all-start.2 = ((bf16[16,160,3200]{2,1,0:T(8,128)(2,1)}), bf16[16,160,3200]{2,1,0:T(8,128)(2,1)}, u32[]{:S(2)}, u32[]{:S(2)}) async-start(bf16[16,160,3200]{2,1,0:T(8,128)(2,1)} %tile.2), calls=%async_computation.2 | async-start | bytes 32768000 | tf_op jit(solution)/shard_map/all_to_all | solution.py:25
  397.4 704.2 %all-to-all-done.2 = bf16[16,160,3200]{2,1,0:T(8,128)(2,1)} async-done(((bf16[16,160,3200]{2,1,0:T(8,128)(2,1)}), bf16[16,160,3200]{2,1,0:T(8,128)(2,1)}, u32[]{:S(2)}, u32[]{:S(2)}) %all-to-all-start.2) | async-done | bytes 16384032 | tf_op jit(solution)/shard_map/all_to_all | solution.py:25
  1101.5 13.8 %fusion.89 = (f32[512]{0:T(512)S(1)}, f32[512,3200]{1,0:T(8,128)S(1)}) fusion(bf16[512,2560]{0,1:T(8,128)(2,1)S(1)} %bitcast.158, bf16[2560,3200]{1,0:T(8,128)(2,1)} %bitcast.24), kind=kOutput, calls=%fused_computation.170 | convolution fusion | flops 8390245888 | bytes 25561088 | tf_op jit(solution)/shard_map/dot_general | solution.py:259
  1117.4 14.2 %all-gather.3 = f32[8,3,512]{2,1,0:T(4,128)S(1)} all-gather(f32[1,3,512]{2,1,0:T(4,128)S(1)} %maximum_bitcast_fusion), channel_id=4, replica_groups=mesh['groups'=2,'seq'=16,'head'=8] {'head'}, dimensions={0}, use_global_device_ids=true | all-gather | bytes 55296 | tf_op jit(solution)/shard_map/all_gather | solution.py:88
  1132.6 21.8 %all_to_all.26 = f32[16,1,16]{2,1,0:T(1,128)S(1)} all-to-all(f32[16,1,16]{2,1,0:T(1,128)S(1)} %broadcast_in_dim.28), channel_id=1, replica_groups=mesh['groups'=2,'seq'=16,'head'=8] {'seq'}, dimensions={0} | all-to-all | bytes 2048 | tf_op jit(solution)/shard_map/all_to_all | solution.py:71
  (194 shorter events, 68.5 us)
Async XLA Ops:
  7.2 229.1 %copy-start = (bf16[640,2560]{1,0:T(8,128)(2,1)S(1)}, bf16[640,2560]{1,0:T(8,128)(2,1)}, u32[]{:S(2)}) copy-start(bf16[640,2560]{1,0:T(8,128)(2,1)} %param.37) | copy-start | bytes 9830404
  7.2 198.9 %all-gather.6.cloned.1.call-start = ((), (), s32[]{:S(2)}) async-start(), calls=%async_computation.4 | async-start | bytes 5570560 | tf_op jit(solution)/shard_map/all_gather | solution.py:40
  8.7 23.2 %collective-permute-start = (bf16[3,640]{1,0:T(4,128)(2,1)}, bf16[3,640]{1,0:T(4,128)(2,1)}, u32[]{:S(2)}, u32[]{:S(2)}) collective-permute-start(bf16[3,640]{1,0:T(4,128)(2,1)} %slice.103), channel_id=1, source_target_pairs={{0,8},{8,16},{16,24},{24,32},{32,40},{40,48},{48,56},{56,64},{64,7... | collective-permute-start | bytes 11528 | tf_op jit(solution)/shard_map/ppermute | solution.py:35
  15.2 14.5 %collective-permute-start.1 = (bf16[3,256]{1,0:T(4,128)(2,1)S(1)}, bf16[3,256]{1,0:T(4,128)(2,1)S(1)}, u32[]{:S(2)}, u32[]{:S(2)}) collective-permute-start(bf16[3,256]{1,0:T(4,128)(2,1)S(1)} %slice.112), channel_id=1, source_target_pairs={{0,8},{8,16},{16,24},{24,32},{32,40},{40,48},{48,56},{56,64},{64,7... | collective-permute-start | bytes 4616 | tf_op jit(solution)/shard_map/ppermute | solution.py:35
  22.9 7.8 copy-start.16
  30.7 1.2 copy-start.9
  31.2 0.7 copy-start.5
  31.2 1.5 copy-start.12
  31.2 1.5 copy-start.13
  31.2 1.5 copy-start.14
  31.2 1.5 copy-start.15
  48.5 3.6 copy-start.3
  58.9 1.4 copy-start.11
  61.8 17.6 %copy-start.4 = (f32[256,10]{0,1:T(8,128)S(1)}, f32[256,10]{0,1:T(8,128)}, u32[]{:S(2)}) copy-start(f32[256,10]{0,1:T(8,128)} %get-tuple-element.606) | copy-start | bytes 30724 | tf_op jit(solution)/shard_map/while
  88.5 3.6 copy-start.3
  98.9 1.4 copy-start.11
  101.9 17.6 %copy-start.4 = (f32[256,10]{0,1:T(8,128)S(1)}, f32[256,10]{0,1:T(8,128)}, u32[]{:S(2)}) copy-start(f32[256,10]{0,1:T(8,128)} %get-tuple-element.606) | copy-start | bytes 30724 | tf_op jit(solution)/shard_map/while
  206.9 0.9 copy-start.6
  206.9 1.0 copy-start.20
  242.5 65.2 %all-to-all-start = ((f32[8,512,320]{1,2,0:T(8,128)}), f32[8,512,320]{1,2,0:T(8,128)}, u32[]{:S(2)}, u32[]{:S(2)}) async-start(f32[8,512,320]{1,2,0:T(8,128)} %bitcast.152), calls=%async_computation | async-start | bytes 10485760 | tf_op jit(solution)/shard_map/all_to_all | solution.py:59
  248.3 62.5 %copy-start.10 = (bf16[512,320]{0,1:T(8,128)(2,1)S(1)}, bf16[512,320]{0,1:T(8,128)(2,1)}, u32[]{:S(2)}) copy-start(bf16[512,320]{0,1:T(8,128)(2,1)} %param.24) | copy-start | bytes 983044
  311.0 12.8 %copy-start.7 = (bf16[512,320]{0,1:T(8,128)(2,1)}, bf16[512,320]{0,1:T(8,128)(2,1)S(1)}, u32[]{:S(2)}) copy-start(bf16[512,320]{0,1:T(8,128)(2,1)S(1)} %get-tuple-element.425) | copy-start | bytes 983044
  324.2 36.1 %copy-start.8 = (bf16[160,3200]{1,0:T(8,128)(2,1)S(1)}, bf16[160,3200]{1,0:T(8,128)(2,1)}, u32[]{:S(2)}) copy-start(bf16[160,3200]{1,0:T(8,128)(2,1)} %param.39) | copy-start | bytes 3072004
  366.1 31.3 %copy-start.19 = (s32[512]{0:T(512)S(1)}, s32[512]{0:T(512)}, u32[]{:S(2)}) copy-start(s32[512]{0:T(512)} %param.40) | copy-start | bytes 6148
  366.1 735.5 %copy-start.2 = (bf16[8,512,320]{1,2,0:T(8,128)(2,1)S(1)}, bf16[8,512,320]{1,2,0:T(8,128)(2,1)}, u32[]{:S(2)}) copy-start(bf16[8,512,320]{1,2,0:T(8,128)(2,1)} %all_to_all.25) | copy-start | bytes 7864324
  366.1 735.5 %all-to-all-start.2 = ((bf16[16,160,3200]{2,1,0:T(8,128)(2,1)}), bf16[16,160,3200]{2,1,0:T(8,128)(2,1)}, u32[]{:S(2)}, u32[]{:S(2)}) async-start(bf16[16,160,3200]{2,1,0:T(8,128)(2,1)} %tile.2), calls=%async_computation.2 | async-start | bytes 32768000 | tf_op jit(solution)/shard_map/all_to_all | solution.py:25
  1115.3 16.9 %copy-start.17 = (s32[512]{0:T(512)S(1)}, s32[512]{0:T(512)}, u32[]{:S(2)}) copy-start(s32[512]{0:T(512)} %copy-done.16) | copy-start | bytes 6148
  1115.3 39.0 %copy-start.18 = (s32[16]{0:T(128)S(1)}, s32[16]{0:T(128)}, u32[]{:S(2)}) copy-start(s32[16]{0:T(128)} %param.41) | copy-start | bytes 196
  1115.3 39.5 %copy-start.1 = (bf16[640,2560]{1,0:T(8,128)(2,1)S(1)}, bf16[640,2560]{1,0:T(8,128)(2,1)}, u32[]{:S(2)}) copy-start(bf16[640,2560]{1,0:T(8,128)(2,1)} %param.37) | copy-start | bytes 9830404
Sparse Core Ops, SparseCore 0:
  121.9 84.1 all-gather.5
